TPU v7x, 32 devices: a whole 2x2x4 slice. The times are simulated.
32 devices in a mesh: seq: 16 (over z, y, x), tp: 2 (over core).
Axes of the slice: x: 2, y: 2, z: 4, core: 2. Of those that a mesh axis runs over, the one named last changes fastest.
Arguments:
- img_qkv: bfloat16 [1, 512, 3, 2048], P(None, 'seq', None, 'tp'), may hold values from -7 to 7
- txt_qkv: bfloat16 [1, 256, 3, 2048], P(None, None, None, 'tp'), may hold values from -7 to 7
- frame_index: int32 [1, 512], P(None, 'seq'), may hold values from 0 to 32
- row_index: int32 [1, 512], P(None, 'seq'), may hold values from 0 to 44
- column_index: int32 [1, 512], P(None, 'seq'), may hold values from 0 to 79
- txt_len: int32 [1], replicated, may hold values from 64 to 256
- residual: bfloat16 [1, 512, 3072], P(None, ('seq', 'tp')), may hold values from -6 to 6
- w_proj: bfloat16 [2048, 3072], P('tp'), may hold values from -0.125 to 0.125
- proj_bias: float32 [3072], replicated, may hold values from -3 to 3
- gate: float32 [3072], replicated, may hold values from -4 to 4
Outputs:
- img_out: bfloat16 [1, 512, 3072], P(None, ('seq', 'tp'))
- txt_out: bfloat16 [1, 256, 2048], P(None, None, 'tp')
All inputs are finite; a program needn't handle non-finite values.
Results may differ from a plain program's by a relative error of at most 0.0082.
Values may be sent and summed in bfloat16 or wider, within the bound.
A program may use at most 64 MiB of HBM per device.

v0:
```python
import functools
import math

import jax
import jax.numpy as jnp
from jax import lax
from jax.experimental import pallas as pl
from jax.experimental.pallas import tpu as pltpu
from jax.sharding import PartitionSpec as P

HD = 128
ROPE_BASE_LOG2 = 8.0
NEG_LARGE = -1e30
F32 = jnp.float32
BF16 = jnp.bfloat16


def largest_divisor(n):
    best = 1
    for d in range(1, n + 1):
        if n % d == 0 and d * d <= n:
            best = d
    return best


def kernel(
    n, heads, img_hbm, txt_hbm, frame_hbm, row_hbm, column_hbm, len_ref, res_hbm, w_hbm, bias_hbm, gate_hbm,
    out_hbm, txt_out_hbm,
    out_ref, txt_out,
    img_ref, txt_q, places, q_send, k_send, q_all, k_all, v_all, a_send, home, t_send, w, res, bias, gate, p_send, p_recv,
    local_sem, q_ss, q_rs, k_ss, k_rs, kr_ss, v_ss, v_rs, vr_ss, a_ss, a_rs, t1_ss, t2_ss, t_rs, p_ss, p_rs,
):
    p = lax.axis_index("seq")
    t = lax.axis_index("tp")
    groups = n // heads
    head = p // groups
    group = p % groups
    tokens = img_ref.shape[1]
    text = txt_hbm.shape[1]
    share = text // groups
    image_keys = n * tokens
    scale = 1.0 / math.sqrt(HD)
    chunks = p_send.shape[0]
    width = p_send.shape[2]
    half = tokens // 2
    plane = largest_divisor(n)
    lines = n // plane

    def rows(s):
        return pl.ds(pl.multiple_of(s * tokens, tokens), tokens)

    def cols(h):
        return pl.ds(pl.multiple_of(h * HD, HD), HD)

    text_rows = pl.ds(pl.multiple_of(group * share, share), share)
    text_keys = pl.ds(image_keys, text)
    early, middle, late = (
        [pltpu.make_async_copy(src, dst, local_sem.at[first + i]) for i, (src, dst) in enumerate(pairs)]
        for first, pairs in (
            (
                0,
                (
                    (frame_hbm, places.at[0]),
                    (row_hbm, places.at[1]),
                    (column_hbm, places.at[2]),
                    (img_hbm, img_ref),
                ),
            ),
            (
                4,
                (
                    (txt_hbm.at[0, text_rows, cols(head)], txt_q),
                    (txt_hbm.at[1, :, cols(head)], k_all.at[text_keys]),
                    (txt_hbm.at[2, :, cols(head)], v_all.at[text_keys]),
                ),
            ),
            (7, ((w_hbm, w), (res_hbm, res), (bias_hbm, bias), (gate_hbm, gate))),
        )
    )
    for load in early + middle + late:
        load.start()

    barrier = pltpu.get_barrier_semaphore()

    def greet(o, carry):
        pl.semaphore_signal(barrier, inc=1, device_id={"seq": (p + o) % n})
        return carry

    lax.fori_loop(1, n, greet, 0)
    pl.semaphore_signal(barrier, inc=1, device_id={"tp": 1 - t})

    diagonal = lax.broadcasted_iota(jnp.int32, (tokens, tokens), 0) == lax.broadcasted_iota(
        jnp.int32, (tokens, tokens), 1
    )
    channel = lax.broadcasted_iota(jnp.int32, (1, HD), 1)
    first = HD // 8
    second = (HD - first) // 2
    angles = jnp.zeros((tokens, HD), F32)
    for load in early:
        load.wait()
    for part, (start, size) in enumerate(
        ((0, first), (first, second), (first + second, second))
    ):
        inside = (channel >= start) & (channel < start + size)
        pair = ((channel - start) // 2).astype(F32)
        rate = jnp.where(inside, jnp.exp2(pair * (-2.0 * ROPE_BASE_LOG2 / size)), 0.0)
        column = jnp.sum(
            jnp.where(diagonal, places[part].astype(F32), 0.0), axis=1, keepdims=True
        )
        angles = angles + column * rate
    even = lax.broadcasted_iota(jnp.int32, (tokens, HD), 1) % 2 == 0
    cosine = jnp.cos(angles)
    sine = jnp.where(even, -1.0, 1.0) * jnp.sin(angles)
    for which, dst in ((0, q_send), (1, k_send)):
        for h in range(heads):
            x = img_ref[which, :, h * HD : (h + 1) * HD].astype(F32)
            partner = jnp.where(even, pltpu.roll(x, HD - 1, 1), pltpu.roll(x, 1, 1))
            dst[h] = (x * cosine + partner * sine).astype(BF16)

    pl.semaphore_wait(barrier, n)

    def q_copy(h, src_line):
        return pltpu.make_async_remote_copy(
            q_send.at[h], q_all.at[rows(src_line)], q_ss.at[h], q_rs.at[src_line],
            device_id={"seq": h * groups + group},
        )

    def k_copy(h, s):
        return pltpu.make_async_remote_copy(
            k_send.at[h], k_all.at[rows(s)], k_ss.at[h], k_rs.at[s],
            device_id={"seq": h * groups + group},
        )

    def v_copy(h, s):
        return pltpu.make_async_remote_copy(
            img_ref.at[2, :, cols(h)], v_all.at[rows(s)], v_ss.at[h], v_rs.at[s],
            device_id={"seq": h * groups + group},
        )

    def k_relay(j, o, s):
        return pltpu.make_async_remote_copy(
            k_all.at[rows(s)], k_all.at[rows(s)], kr_ss.at[j, o], k_rs.at[s],
            device_id={"seq": head * groups + (group + o) % groups},
        )

    def v_relay(j, o, s):
        return pltpu.make_async_remote_copy(
            v_all.at[rows(s)], v_all.at[rows(s)], vr_ss.at[j, o], v_rs.at[s],
            device_id={"seq": head * groups + (group + o) % groups},
        )

    def a_copy(j, h):
        return pltpu.make_async_remote_copy(
            a_send.at[rows(j)], home.at[:, cols(h)], a_ss.at[j], a_rs.at[h],
            device_id={"seq": j * groups + group},
        )

    def over(count, f):
        def step(o, carry):
            f(o)
            return carry

        lax.fori_loop(1, count, step, 0)

    over(heads, lambda o: k_copy((head + o) % heads, p).start())
    k_all[rows(p), :] = k_send[head]
    over(groups, lambda o: k_relay(head, o, p).start())
    over(heads, lambda o: v_copy((head + o) % heads, p).start())
    v_all[rows(p), :] = img_ref[2, :, cols(head)]
    over(groups, lambda o: v_relay(head, o, p).start())
    over(heads, lambda o: q_copy((head + o) % heads, head).start())
    q_all[rows(head), :] = q_send[head]

    def pass_on(copy, relay):
        def one(o):
            j = (head + heads - o) % heads
            s = j * groups + group
            copy((head + o) % heads, s).wait_recv()
            over(groups, lambda g: relay(j, g, s).start())

        over(heads, one)

    def arrive(relay):
        def one(o):
            def from_line(j, carry):
                relay(j, o, j * groups + (group + o) % groups).wait_recv()
                return carry

            lax.fori_loop(0, heads, from_line, 0)

        over(groups, one)

    pass_on(k_copy, k_relay)
    pass_on(v_copy, v_relay)
    for load in middle:
        load.wait()
    length = len_ref[0]

    def weigh(queries):
        scores = lax.dot_general(
            queries, k_all[...], (((1,), (1,)), ((), ())), preferred_element_type=F32
        )
        live = lax.broadcasted_iota(jnp.int32, scores.shape, 1) < image_keys + length
        scores = jnp.where(live, scores, NEG_LARGE)
        peak = jnp.max(scores, axis=1, keepdims=True)
        weights = jnp.where(live, jnp.exp((scores - peak) * scale), 0.0)
        return weights.astype(BF16), jnp.sum(weights, axis=1, keepdims=True)

    def blend(weights, total):
        return jnp.dot(weights, v_all[...], preferred_element_type=F32) / total

    arrive(k_relay)
    text_weights, text_total = weigh(txt_q[...])
    over(heads, lambda o: q_copy((head + o) % heads, (head + heads - o) % heads).wait_recv())
    image_weights, image_total = weigh(q_all[...])
    arrive(v_relay)
    text_done = blend(text_weights, text_total)
    text_row = lax.broadcasted_iota(jnp.int32, text_done.shape, 0) + group * share
    text_done = jnp.where(text_row < length, text_done, 0.0).astype(BF16)

    def block(s):
        return txt_out.at[
            pl.ds(pl.multiple_of((s % groups) * share, share), share), cols(s // groups)
        ]

    def line_copy(o, s):
        return pltpu.make_async_remote_copy(
            t_send, block(s), t1_ss.at[o], t_rs.at[s], device_id={"seq": (p + o * plane) % n}
        )

    def plane_copy(i, o, s):
        source = t_send if i is None else block(s)
        slot = 0 if i is None else i
        return pltpu.make_async_remote_copy(
            source, block(s), t2_ss.at[slot, o], t_rs.at[s],
            device_id={"seq": (p // plane) * plane + (p % plane + o) % plane},
        )

    t_send[...] = text_done
    txt_out[pl.ds(pl.multiple_of(group * share, share), share), cols(head)] = text_done
    over(lines, lambda o: line_copy(o, p).start())
    over(plane, lambda o: plane_copy(None, o, p).start())

    a_send[...] = blend(image_weights, image_total).astype(BF16)
    over(heads, lambda o: a_copy((head + o) % heads, head).start())
    home[:, cols(head)] = a_send[rows(head), :]

    def forward(i):
        s = (p + n - i * plane) % n
        line_copy(i, s).wait_recv()
        over(plane, lambda o: plane_copy(i, o, s).start())

    over(lines, forward)

    over(heads, lambda o: a_copy((head + o) % heads, (head + heads - o) % heads).wait_recv())
    for load in late:
        load.wait()

    def p_copy(c):
        return pltpu.make_async_remote_copy(
            p_send.at[c], p_recv.at[c], p_ss.at[c], p_rs.at[c], device_id={"tp": 1 - t}
        )

    mine = []
    for c in range(chunks):
        part = jnp.dot(home[...], w[:, c * width : (c + 1) * width], preferred_element_type=F32)
        top, bottom = part[:half], part[half:]
        p_send[c] = jnp.where(t == 0, bottom, top).astype(BF16)
        p_copy(c).start()
        at = slice(c * width, (c + 1) * width)
        mine.append(jnp.where(t == 0, top, bottom))
    def finish_plane(o):
        def one(i, carry):
            s = i * plane + (p % plane + o) % plane
            plane_copy(None, o, s).wait_recv()
            return carry

        lax.fori_loop(0, lines, one, 0)
        plane_copy(None, o, p).wait_send()

    over(plane, finish_plane)
    stores = [
        pltpu.make_async_copy(src, dst, local_sem.at[11 + i])
        for i, (src, dst) in enumerate(((txt_out, txt_out_hbm), (out_ref, out_hbm)))
    ]
    stores[0].start()
    for c in range(chunks):
        at = slice(c * width, (c + 1) * width)
        p_copy(c).wait_recv()
        projected = mine[c] + p_recv[c].astype(F32)
        out_ref[:, at] = (
            res[:, at].astype(F32) + gate[:, at] * (projected + bias[:, at])
        ).astype(BF16)
    stores[1].start()

    def finish_line(i):
        s = (p + n - i * plane) % n
        over(plane, lambda o: plane_copy(i, o, s).wait_send())
        line_copy(i, s).wait_send()

    over(lines, finish_line)
    def finish_relay(relay):
        def one(o):
            def to_line(j, carry):
                relay(j, o, j * groups + group).wait_send()
                return carry

            lax.fori_loop(0, heads, to_line, 0)

        over(groups, one)

    finish_relay(k_relay)
    finish_relay(v_relay)
    over(heads, lambda o: k_copy((head + o) % heads, p).wait_send())
    over(heads, lambda o: v_copy((head + o) % heads, p).wait_send())
    over(heads, lambda o: q_copy((head + o) % heads, head).wait_send())
    over(heads, lambda o: a_copy((head + o) % heads, head).wait_send())
    for c in range(chunks):
        p_copy(c).wait_send()
    for copy in stores:
        copy.wait()


def store(img_in, txt_in, img_out, txt_out, img, txt, load_sem, store_sem):
    pieces = load_sem.shape[0] - 1
    rows = txt.shape[0] // pieces
    parts = [(txt_in.at[pl.ds(i * rows, rows)], txt.at[pl.ds(i * rows, rows)],
              txt_out.at[0, pl.ds(i * rows, rows)]) for i in range(pieces)]
    parts.append((img_in, img, img_out.at[0]))
    loads = [pltpu.make_async_copy(a, b, load_sem.at[i]) for i, (a, b, c) in enumerate(parts)]
    stores = [pltpu.make_async_copy(b, c, store_sem.at[i]) for i, (a, b, c) in enumerate(parts)]
    for load in loads:
        load.start()
    for load, put in zip(loads, stores):
        load.wait()
        put.start()
    for put in stores:
        put.wait()


def shards(img_qkv, txt_qkv, frame_index, row_index, column_index, txt_len, residual, w_proj, proj_bias, gate):
    tokens = img_qkv.shape[1]
    channels = img_qkv.shape[3]
    heads = channels // HD
    n = lax.axis_size("seq")
    groups = n // heads
    text = txt_qkv.shape[1]
    share = text // groups
    plane = largest_divisor(n)
    lines = n // plane
    model = w_proj.shape[1]
    half = residual.shape[1]
    chunks = 4
    img = img_qkv[0].transpose(1, 0, 2)
    txt = txt_qkv[0].transpose(1, 0, 2)
    hbm = pl.BlockSpec(memory_space=pltpu.HBM)
    dma = pltpu.SemaphoreType.DMA
    out, txt_out = pl.pallas_call(
        functools.partial(kernel, n, heads),
        out_shape=(
            jax.ShapeDtypeStruct((half, model), BF16),
            jax.ShapeDtypeStruct((text, channels), BF16),
        ),
        in_specs=[hbm] * 5 + [pl.BlockSpec(memory_space=pltpu.SMEM)] + [hbm] * 4,
        out_specs=(hbm, hbm),
        scratch_shapes=[
            pltpu.VMEM((half, model), BF16),
            pltpu.VMEM((text, channels), BF16),
            pltpu.VMEM((3, tokens, channels), BF16),
            pltpu.VMEM((share, HD), BF16),
            pltpu.VMEM((3, 1, tokens), jnp.int32),
            pltpu.VMEM((heads, tokens, HD), BF16),
            pltpu.VMEM((heads, tokens, HD), BF16),
            pltpu.VMEM((heads * tokens, HD), BF16),
            pltpu.VMEM((n * tokens + text, HD), BF16),
            pltpu.VMEM((n * tokens + text, HD), BF16),
            pltpu.VMEM((heads * tokens, HD), BF16),
            pltpu.VMEM((tokens, channels), BF16),
            pltpu.VMEM((share, HD), BF16),
            pltpu.VMEM(w_proj.shape, BF16),
            pltpu.VMEM((half, model), BF16),
            pltpu.VMEM((1, model), F32),
            pltpu.VMEM((1, model), F32),
            pltpu.VMEM((chunks, half, model // chunks), BF16),
            pltpu.VMEM((chunks, half, model // chunks), BF16),
            dma((13,)),
            dma((heads,)), dma((heads,)),
            dma((heads,)), dma((n,)), dma((heads, groups)),
            dma((heads,)), dma((n,)), dma((heads, groups)),
            dma((heads,)), dma((heads,)),
            dma((lines,)), dma((lines, plane)), dma((n,)),
            dma((chunks,)), dma((chunks,)),
        ],
        compiler_params=pltpu.CompilerParams(
            collective_id=0, has_side_effects=True, vmem_limit_bytes=67043328
        ),
    )(
        img, txt, frame_index, row_index, column_index, txt_len, residual[0], w_proj,
        proj_bias[None], gate[None],
    )
    return pl.pallas_call(
        store,
        out_shape=(
            jax.ShapeDtypeStruct((1,) + out.shape, BF16),
            jax.ShapeDtypeStruct((1,) + txt_out.shape, BF16),
        ),
        in_specs=[hbm, hbm],
        out_specs=(hbm, hbm),
        scratch_shapes=[
            pltpu.VMEM(out.shape, BF16), pltpu.VMEM(txt_out.shape, BF16), dma((5,)), dma((5,)),
        ],
        compiler_params=pltpu.CompilerParams(vmem_limit_bytes=66400000),
    )(out, txt_out)


def solution(mesh):
    in_specs = (
        P(None, "seq", None, "tp"),
        P(None, None, None, "tp"),
        P(None, "seq"),
        P(None, "seq"),
        P(None, "seq"),
        P(),
        P(None, ("seq", "tp"), None),
        P("tp", None),
        P(),
        P(),
    )
    out_specs = (P(None, ("seq", "tp"), None), P(None, None, "tp"))
    return jax.shard_map(shards, mesh=mesh, in_specs=in_specs, out_specs=out_specs, check_vma=False)
```

profile of v0, /device:TPU:0, one launch (start us, length us, event | category | flops | bytes accessed | tf_op | source)
XLA Modules:
  0.0 29.9 jit_solution(9785776501979019351)
XLA Ops:
  1.3 26.8 %shard_map.113 = (bf16[16,3072]{1,0:T(8,128)(2,1)}, bf16[256,1024]{1,0:T(8,128)(2,1)}) custom-call(bf16[3,32,1024]{2,1,0:T(8,128)(2,1)} %bitcast.10, bf16[3,256,1024]{2,1,0:T(8,128)(2,1)} %bitcast.9, s32[1,32]{1,0:T(1,128)} %frame_hbm.1, s32[1,32]{1,0:T(1,128)} %row_hbm.1, s32[1,32]{1,0:T(1,128)} %column_hbm.1, s32[1]{0:T(128)S(6)} %copy.12.len_ref, ...), custom_call_target="tpu_custom_call" | custom-call | tf_op jit(solution)/shard_map/pallas_call | solution.py:358
  28.0 1.9 %shard_map.114 = (bf16[1,16,3072]{2,1,0:T(8,128)(2,1)}, bf16[1,256,1024]{2,1,0:T(8,128)(2,1)}) custom-call(bf16[16,3072]{1,0:T(8,128)(2,1)} %get-tuple-element.4.img_in, bf16[256,1024]{1,0:T(8,128)(2,1)} %get-tuple-element.5.txt_in), custom_call_target="tpu_custom_call" | custom-call | tf_op jit(solution)/shard_map/pallas_call | solution.py:401
where the time goes:
time: 30.1 us; the launch traced here: 29.9 us
  Pallas kernels  28.6 us (95%)
  between operations  1.29 us (4%)
    pallas_call x1, Pallas kernels, shards(): pl.pallas_call(functools.partial(kernel, n, heads), out_shape=(jax.ShapeD...  26.8 us
    pallas_call x1, Pallas kernels, shards(): pl.pallas_call(store, out_shape=(jax.ShapeDtypeStruct((1,) + out.shape, B...  1.88 us

commit v1 on v0

v1 whole, which is shorter than its diff:
```python
import functools
import math

import jax
import jax.numpy as jnp
from jax import lax
from jax.experimental import pallas as pl
from jax.experimental.pallas import tpu as pltpu
from jax.sharding import PartitionSpec as P

HD = 128
ROPE_BASE_LOG2 = 8.0
NEG_LARGE = -1e30
F32 = jnp.float32
BF16 = jnp.bfloat16
LOADS = 11
DIRECT = (0, 1, 2, 3)


def largest_divisor(n):
    best = 1
    for d in range(1, n + 1):
        if n % d == 0 and d * d <= n:
            best = d
    return best


def over(start, count, f):
    if count - start <= 8:
        for o in range(start, count):
            f(o)
    else:
        lax.fori_loop(start, count, lambda o, c: (f(o), c)[1], 0)


class Ring:
    def __init__(self, index, count):
        self.index, self.count = index, count
        self.paired = count & (count - 1) == 0
        self.flips = []
        if self.paired:
            bit = 1
            while bit < count:
                self.flips.append((bit, (1 - 2 * ((index // bit) % 2)) * bit))
                bit *= 2

    def meet(self, o, sign):
        if not self.paired:
            return (self.index + sign * o + self.count) % self.count
        total = self.index
        for bit, flip in self.flips:
            if isinstance(o, int):
                total = total + flip if o & bit else total
            else:
                total = total + flip * ((o // bit) % 2)
        return total

    def to(self, o):
        return self.meet(o, 1)

    def source(self, o):
        return self.meet(o, -1)


def kernel(
    n, heads, img_hbm, txt_hbm, frame_hbm, row_hbm, column_hbm, len_ref, res_hbm, w_hbm, bias_hbm, gate_hbm,
    out_ref, txt_out,
    img_ref, txt_q, places, q_send, k_send, q_all, k_all, v_all, a_send, home, t_send, w, res, bias, gate, total, p_send,
    p_recv, load_sem, k_ss, v_ss, q_ss, kr_ss, vr_ss, a_ss, p_ss, t_ss, k_rs, v_rs, q_rs, kr_rs, vr_rs, a_rs, t1_rs, t2_rs,
    t3_rs, p_rs,
):
    p = lax.axis_index("seq")
    t = lax.axis_index("tp")
    groups = n // heads
    head = p // groups
    group = p % groups
    tokens = img_ref.shape[1]
    text = txt_hbm.shape[1]
    share = text // groups
    plane_keys = heads * tokens
    early_keys = plane_keys + text
    scale = 1.0 / math.sqrt(HD)
    chunks = p_send.shape[0]
    width = p_send.shape[2]
    half = tokens // 2
    plane = largest_divisor(n)
    lines = n // plane
    inner = largest_divisor(plane)
    outer = plane // inner
    line = p // plane
    v = p % inner
    u = (p // inner) % outer
    direct = [o for o in DIRECT if o < lines]
    near = plane % groups == 0 and groups % inner == 0 and inner % groups == 0
    by_head, by_group = Ring(head, heads), Ring(group, groups)
    by_line, by_u, by_v = Ring(line, lines), Ring(u, outer), Ring(v, inner)
    joined = 2 if by_head.paired and heads % 2 == 0 else heads
    pairs = heads // joined
    by_pair = Ring(head // joined, pairs)

    def rows(first, count):
        return pl.ds(pl.multiple_of(first, count), count)

    def cols(h):
        return pl.ds(pl.multiple_of(h * HD, HD), HD)

    def plane_slot(j):
        return rows(j * tokens, tokens)

    def relay_slot(o, j):
        return pl.ds(pl.multiple_of(early_keys + ((o - 1) * heads + j) * tokens, tokens), tokens)

    def remote(src, dst, send, recv, where):
        return pltpu.make_async_remote_copy(src, dst, send, recv, device_id=where)

    barrier = pltpu.get_barrier_semaphore()

    def greet(where):
        pl.semaphore_signal(barrier, inc=1, device_id=where)

    if near:
        over(1, heads, lambda o: greet({"seq": by_head.to(heads - o) * groups + group}))
        over(1, groups, lambda o: greet({"seq": head * groups + by_group.to(o)}))
        greetings = heads + groups - 1
        if direct:
            for i in range(1, outer):
                over(1, inner, lambda o, i=i: greet({"seq": line * plane + by_u.to(i) * inner + by_v.to(o)}))
            greetings += (outer - 1) * (inner - 1)
    else:
        over(1, n, lambda o: greet({"seq": (p + o) % n}))
        greetings = n
    greet({"tp": 1 - t})

    own_text = rows(group * share, share)
    text_keys = pl.ds(plane_keys, text)
    loads = [
        pltpu.make_async_copy(src, dst, load_sem.at[i])
        for i, (src, dst) in enumerate(
            (
                (frame_hbm, places.at[0]),
                (row_hbm, places.at[1]),
                (column_hbm, places.at[2]),
                (img_hbm, img_ref),
                (txt_hbm.at[0, own_text, cols(head)], txt_q),
                (txt_hbm.at[1, :, cols(head)], k_all.at[text_keys]),
                (txt_hbm.at[2, :, cols(head)], v_all.at[text_keys]),
                (w_hbm, w),
                (res_hbm, res),
                (bias_hbm, bias),
                (gate_hbm, gate),
            )
        )
    ]
    for load in loads:
        load.start()

    diagonal = lax.broadcasted_iota(jnp.int32, (tokens, tokens), 0) == lax.broadcasted_iota(
        jnp.int32, (tokens, tokens), 1
    )
    channel = lax.broadcasted_iota(jnp.int32, (1, HD), 1)
    first = HD // 8
    second = (HD - first) // 2
    angles = jnp.zeros((tokens, HD), F32)
    for load in loads[:4]:
        load.wait()
    for part, (start, size) in enumerate(
        ((0, first), (first, second), (first + second, second))
    ):
        inside = (channel >= start) & (channel < start + size)
        pair = ((channel - start) // 2).astype(F32)
        rate = jnp.where(inside, jnp.exp2(pair * (-2.0 * ROPE_BASE_LOG2 / size)), 0.0)
        column = jnp.sum(
            jnp.where(diagonal, places[part].astype(F32), 0.0), axis=1, keepdims=True
        )
        angles = angles + column * rate
    even = lax.broadcasted_iota(jnp.int32, (tokens, HD), 1) % 2 == 0
    cosine = jnp.cos(angles)
    sine = jnp.where(even, -1.0, 1.0) * jnp.sin(angles)
    for which, dst in ((1, k_send), (0, q_send)):
        for h in range(heads):
            x = img_ref[which, :, h * HD : (h + 1) * HD].astype(F32)
            partner = jnp.where(even, pltpu.roll(x, HD - 1, 1), pltpu.roll(x, 1, 1))
            dst[h] = (x * cosine + partner * sine).astype(BF16)
    k_all[plane_slot(head), :] = k_send[head]
    v_all[plane_slot(head), :] = img_ref[2, :, cols(head)]
    q_all[plane_slot(head), :] = q_send[head]

    pl.semaphore_wait(barrier, greetings)

    def line_up(h):
        return {"seq": h * groups + group}

    def k_copy(o, h, j):
        return remote(k_send.at[h], k_all.at[plane_slot(j)], k_ss, k_rs.at[o], line_up(h))

    def v_copy(o, h, j):
        return remote(img_ref.at[2, :, cols(h)], v_all.at[plane_slot(j)], v_ss, v_rs.at[o], line_up(h))

    def q_copy(h):
        return remote(q_send.at[h], q_all.at[plane_slot(head)], q_ss, q_rs, line_up(h))

    def relay(data, send, recv, j):
        def one(o):
            g = by_group.to(o)
            remote(
                data.at[plane_slot(j)], data.at[relay_slot(o, j)], send, recv, {"seq": head * groups + g}
            ).start()

        over(1, groups, one)

    def all_of(count, send, recv):
        wide = -(-count // k_all.shape[0])
        block = k_all.at[pl.ds(0, count)] if wide == 1 else w.at[pl.ds(0, count * HD // w.shape[1])]
        return remote(block, block, send, recv, {"tp": 1 - t})

    relay(k_all, kr_ss, kr_rs, head)
    over(1, heads, lambda o: k_copy(o, by_head.to(o), head).start())
    relay(v_all, vr_ss, vr_rs, head)
    over(1, heads, lambda o: v_copy(o, by_head.to(o), head).start())
    over(1, heads, lambda o: q_copy(by_head.to(o)).start())

    def pass_on(copy, data, send, recv):
        def one(o):
            j = by_head.source(o)
            copy(o, head, j).wait_recv()
            relay(data, send, recv, j)

        over(1, heads, one)

    pass_on(k_copy, k_all, kr_ss, kr_rs)
    pass_on(v_copy, v_all, vr_ss, vr_rs)
    for load in loads[4:7]:
        load.wait()
    length = len_ref[0]
    relayed = (groups - 1) * plane_keys

    def scores_of(queries, start, count):
        return lax.dot_general(
            queries, k_all[pl.ds(start, count), :], (((1,), (1,)), ((), ())), preferred_element_type=F32
        )

    def early_scores(queries):
        scores = scores_of(queries, 0, early_keys)
        live = lax.broadcasted_iota(jnp.int32, scores.shape, 1) < plane_keys + length
        return jnp.where(live, scores, NEG_LARGE)

    def weigh(queries, scores):
        peak = jnp.max(scores, axis=1, keepdims=True)
        parts = [scores]
        if relayed:
            parts.append(scores_of(queries, early_keys, relayed))
            peak = jnp.maximum(peak, jnp.max(parts[1], axis=1, keepdims=True))
        live = lax.broadcasted_iota(jnp.int32, scores.shape, 1) < plane_keys + length
        weights = [jnp.exp((part - peak) * scale) for part in parts]
        weights[0] = jnp.where(live, weights[0], 0.0)
        whole = sum(jnp.sum(part, axis=1, keepdims=True) for part in weights)
        return [part.astype(BF16) for part in weights], whole

    def blend(weights, whole):
        mixed = jnp.dot(weights[0], v_all[pl.ds(0, early_keys), :], preferred_element_type=F32)
        if relayed:
            mixed = mixed + jnp.dot(weights[1], v_all[pl.ds(early_keys, relayed), :], preferred_element_type=F32)
        return mixed / whole

    text_scores = early_scores(txt_q[...])
    if heads > 1:
        all_of((heads - 1) * tokens, q_ss, q_rs).wait_recv()
    if relayed:
        all_of(relayed, kr_ss, kr_rs).wait_recv()
    text_weights, text_total = weigh(txt_q[...], text_scores)
    image_weights, image_total = weigh(q_all[...], early_scores(q_all[...]))
    if relayed:
        all_of(relayed, vr_ss, vr_rs).wait_recv()
    text_done = blend(text_weights, text_total)
    text_row = lax.broadcasted_iota(jnp.int32, text_done.shape, 0) + group * share
    text_done = jnp.where(text_row < length, text_done, 0.0).astype(BF16)

    def place(l, uu, vv):
        return l * plane + uu * inner + vv

    def block(s):
        return txt_out.at[rows((s % groups) * share, share), cols(s // groups)]

    def line_copy(o, to, s):
        return remote(t_send, block(s), t_ss.at[0], t1_rs.at[o], {"seq": place(to, u, v)})

    def along(ring, at):
        return [(o, at(ring.to(o)), at(ring.source(o))) for o in range(1, ring.count)]

    along_v = along(by_v, lambda x: (u, x))
    along_u = along(by_u, lambda x: (x, v))

    def cross(o, l, own):
        way = o % 2
        first_way, last_way = ((along_v, along_u), (along_u, along_v))[way]
        s = place(l, u, v)
        source = t_send if own else block(s)
        if o in direct:
            corner = [(0, (by_u.to(i), by_v.to(k)), 0) for i in range(1, outer) for k in range(1, inner)]
            for i, to, _ in first_way + last_way + corner:
                remote(source, block(s), t_ss.at[5], t3_rs.at[2], {"seq": place(line, *to)}).start()
            return
        for i, to, _ in first_way:
            remote(source, block(s), t_ss.at[1 + way], t2_rs.at[o, i], {"seq": place(line, *to)}).start()
        for i, to, _ in last_way:
            remote(source, block(s), t_ss.at[3 + way], t3_rs.at[way], {"seq": place(line, *to)}).start()

    def cross_on(o, l):
        if o in direct:
            return
        way = o % 2
        first_way, last_way = ((along_v, along_u), (along_u, along_v))[way]
        for i, _, origin in first_way:
            s = place(l, *origin)
            remote(block(s), block(s), t_ss.at[1 + way], t2_rs.at[o, i], {"tp": 1 - t}).wait_recv()
            for _, to, _ in last_way:
                remote(block(s), block(s), t_ss.at[3 + way], t3_rs.at[way], {"seq": place(line, *to)}).start()

    t_send[...] = text_done
    txt_out[own_text, cols(head)] = text_done
    over(1, lines, lambda o: line_copy(o, by_line.to(o), p).start())

    a_send[...] = blend(image_weights, image_total).astype(BF16)
    home[:, cols(head)] = a_send[plane_slot(head), :]

    def a_send_to(o):
        j = by_head.to(o)
        remote(a_send.at[plane_slot(j)], home.at[:, cols(head)], a_ss, a_rs.at[o // joined], line_up(j)).start()

    over(1, heads, a_send_to)
    cross(0, line, True)

    def receive_pair(o):
        count = joined * tokens - (tokens if o == 0 else 0)
        if count:
            all_of(count, a_ss, a_rs.at[o]).wait_recv()

    def project(o):
        receive_pair(o)
        at = rows(by_pair.to(o) * joined * HD, joined * HD)
        return [
            jnp.dot(home[:, at], w[at, c * width : (c + 1) * width], preferred_element_type=F32)
            for c in range(chunks)
        ]

    def p_copy(c):
        return remote(p_send.at[c], p_recv.at[c], p_ss, p_rs.at[c], {"tp": 1 - t})

    def step(o):
        if o == 0:
            cross_on(0, line)
        else:
            l = by_line.source(o)
            remote(block(p), block(p), t_ss.at[0], t1_rs.at[o], {"tp": 1 - t}).wait_recv()
            cross(o, l, False)

    def keep(o):
        for c, part in enumerate(project(o)):
            at = slice(c * width, (c + 1) * width)
            total[:, at] = part if o == 0 else total[:, at] + part

    for load in loads[7:]:
        load.wait()
    for o in range(lines):
        step(o)
    for o in range(1, lines):
        cross_on(o, by_line.source(o))
    for o in range(pairs - 1):
        keep(o)
    last = project(pairs - 1)
    mine = []
    for c in range(chunks):
        at = slice(c * width, (c + 1) * width)
        part = last[c] if pairs == 1 else total[:, at] + last[c]
        top, bottom = part[:half], part[half:]
        p_send[c] = jnp.where(t == 0, bottom, top).astype(BF16)
        p_copy(c).start()
        mine.append(jnp.where(t == 0, top, bottom))
    for c in range(chunks):
        at = slice(c * width, (c + 1) * width)
        p_copy(c).wait_recv()
        projected = mine[c] + p_recv[c].astype(F32)
        out_ref[:, at] = (
            res[:, at].astype(F32) + gate[:, at] * (projected + bias[:, at])
        ).astype(BF16)

    def finish(count, sem):
        if count:
            all_of(count, sem, sem).wait_send()

    counts = [sum(o % 2 == way and o not in direct for o in range(lines)) for way in (0, 1)]
    spread = len(direct) * (plane - 1) * share
    if spread:
        all_of(spread, t_ss.at[0], t3_rs.at[2]).wait_recv()
    for way, (one, two) in enumerate(((inner, outer), (outer, inner))):
        if counts[way] and two > 1:
            all_of(counts[way] * one * (two - 1) * share, t_ss.at[0], t3_rs.at[way]).wait_recv()
    finish((heads - 1) * tokens, k_ss)
    finish((heads - 1) * tokens, v_ss)
    finish((heads - 1) * tokens, q_ss)
    finish((heads - 1) * tokens, a_ss)
    finish(relayed, kr_ss)
    finish(relayed, vr_ss)
    finish((lines - 1) * share, t_ss.at[0])
    for way, (one, two) in enumerate(((inner, outer), (outer, inner))):
        finish(counts[way] * (one - 1) * share, t_ss.at[1 + way])
        finish(counts[way] * one * (two - 1) * share, t_ss.at[3 + way])
    finish(spread, t_ss.at[5])
    remote(p_send, p_recv, p_ss, p_rs.at[0], {"tp": 1 - t}).wait_send()


def store(img, txt, img_out, txt_out, store_sem):
    stores = [
        pltpu.make_async_copy(a, b.at[0], store_sem.at[i]) for i, (a, b) in enumerate(((txt, txt_out), (img, img_out)))
    ]
    for put in stores:
        put.start()
    for put in stores:
        put.wait()


def shards(img_qkv, txt_qkv, frame_index, row_index, column_index, txt_len, residual, w_proj, proj_bias, gate):
    tokens = img_qkv.shape[1]
    channels = img_qkv.shape[3]
    heads = channels // HD
    n = lax.axis_size("seq")
    groups = n // heads
    text = txt_qkv.shape[1]
    share = text // groups
    plane = largest_divisor(n)
    lines = n // plane
    inner = largest_divisor(plane)
    outer = plane // inner
    model = w_proj.shape[1]
    half = residual.shape[1]
    chunks = 4
    img = img_qkv[0].transpose(1, 0, 2)
    txt = txt_qkv[0].transpose(1, 0, 2)
    hbm = pl.BlockSpec(memory_space=pltpu.HBM)
    vmem = pl.BlockSpec(memory_space=pltpu.VMEM)
    dma = pltpu.SemaphoreType.DMA
    done = pl.pallas_call(
        functools.partial(kernel, n, heads),
        out_shape=(pltpu.VMEM((half, model), BF16), pltpu.VMEM((text, channels), BF16)),
        in_specs=[hbm] * 5 + [pl.BlockSpec(memory_space=pltpu.SMEM)] + [hbm] * 4,
        out_specs=(vmem, vmem),
        scratch_shapes=[
            pltpu.VMEM((3, tokens, channels), BF16),
            pltpu.VMEM((share, HD), BF16),
            pltpu.VMEM((3, 1, tokens), jnp.int32),
            pltpu.VMEM((heads, tokens, HD), BF16),
            pltpu.VMEM((heads, tokens, HD), BF16),
            pltpu.VMEM((heads * tokens, HD), BF16),
            pltpu.VMEM((n * tokens + text, HD), BF16),
            pltpu.VMEM((n * tokens + text, HD), BF16),
            pltpu.VMEM((heads * tokens, HD), BF16),
            pltpu.VMEM((tokens, channels), BF16),
            pltpu.VMEM((share, HD), BF16),
            pltpu.VMEM(w_proj.shape, BF16),
            pltpu.VMEM((half, model), BF16),
            pltpu.VMEM((1, model), F32),
            pltpu.VMEM((1, model), F32),
            pltpu.VMEM((tokens, model), F32),
            pltpu.VMEM((chunks, half, model // chunks), BF16),
            pltpu.VMEM((chunks, half, model // chunks), BF16),
            dma((LOADS,)),
            dma, dma, dma, dma, dma, dma, dma, dma((6,)),
            dma((heads,)), dma((heads,)), dma, dma, dma,
            dma((heads,)), dma((lines,)), dma((lines, max(inner, outer))), dma((3,)), dma((chunks,)),
        ],
        compiler_params=pltpu.CompilerParams(
            collective_id=0, has_side_effects=True, vmem_limit_bytes=60000000
        ),
    )(
        img, txt, frame_index, row_index, column_index, txt_len, residual[0], w_proj,
        proj_bias[None], gate[None],
    )
    out, txt_out = (pltpu.with_memory_space_constraint(x, pltpu.VMEM) for x in done)
    return pl.pallas_call(
        store,
        out_shape=(
            jax.ShapeDtypeStruct((1,) + out.shape, BF16),
            jax.ShapeDtypeStruct((1,) + txt_out.shape, BF16),
        ),
        in_specs=[vmem, vmem],
        out_specs=(hbm, hbm),
        scratch_shapes=[dma((2,))],
        compiler_params=pltpu.CompilerParams(vmem_limit_bytes=8000000),
    )(out, txt_out)


def solution(mesh):
    in_specs = (
        P(None, "seq", None, "tp"),
        P(None, None, None, "tp"),
        P(None, "seq"),
        P(None, "seq"),
        P(None, "seq"),
        P(),
        P(None, ("seq", "tp"), None),
        P("tp", None),
        P(),
        P(),
    )
    out_specs = (P(None, ("seq", "tp"), None), P(None, None, "tp"))
    return jax.shard_map(shards, mesh=mesh, in_specs=in_specs, out_specs=out_specs, check_vma=False)
```

time: 30.1 us -> 25.8 us (0.86)
  Pallas kernels: 28.6 us -> 24.4 us
    pallas_call x1, Pallas kernels: 26.8 us -> 23.5 us  [shards(): pl.pallas_call(functools.partial(kernel, n, heads), out_shape=(pltpu.VMEM...]
    pallas_call x1, Pallas kernels: 1.88 us -> 0.83 us  [shards(): pl.pallas_call(store, out_shape=(jax.ShapeDtypeStruct((1,) + out.shape, B...]
where the time goes in v1:
time: 25.8 us; the launch traced here: 25.7 us
  Pallas kernels  24.4 us (95%)
  between operations  1.29 us (5%)
    pallas_call x1, Pallas kernels, shards(): pl.pallas_call(functools.partial(kernel, n, heads), out_shape=(pltpu.VMEM...  23.5 us
    pallas_call x1, Pallas kernels, shards(): pl.pallas_call(store, out_shape=(jax.ShapeDtypeStruct((1,) + out.shape, B...  0.83 us

profile of v1, /device:TPU:0, one launch (start us, length us, event | category | flops | bytes accessed | tf_op | source)
XLA Modules:
  0.0 25.7 jit_solution(6570733728172007054)
XLA Ops:
  1.3 23.5 %shard_map.113 = (bf16[16,3072]{1,0:T(8,128)(2,1)S(1)}, bf16[256,1024]{1,0:T(8,128)(2,1)S(1)}) custom-call(bf16[3,32,1024]{2,1,0:T(8,128)(2,1)} %bitcast.10, bf16[3,256,1024]{2,1,0:T(8,128)(2,1)} %bitcast.9, s32[1,32]{1,0:T(1,128)} %frame_hbm.1, s32[1,32]{1,0:T(1,128)} %row_hbm.1, s32[1,32]{1,0:T(1,128)} %column_hbm.1, s32[1]{0:T(128)S(6)} %copy.12.len_ref, ...), custom_call_target="tpu_custom_call" | custom-call | tf_op jit(solution)/shard_map/pallas_call | solution.py:442
  24.8 0.8 %shard_map.114 = (bf16[1,16,3072]{2,1,0:T(8,128)(2,1)}, bf16[1,256,1024]{2,1,0:T(8,128)(2,1)}) custom-call(bf16[16,3072]{1,0:T(8,128)(2,1)S(1)} %get-tuple-element.4.img, bf16[256,1024]{1,0:T(8,128)(2,1)S(1)} %get-tuple-element.5.txt), custom_call_target="tpu_custom_call" | custom-call | tf_op jit(solution)/shard_map/pallas_call | solution.py:479

commit v2 on v1

v2 whole, which is shorter than its diff:
```python
import functools
import math

import jax
import jax.numpy as jnp
from jax import lax
from jax.experimental import pallas as pl
from jax.experimental.pallas import tpu as pltpu
from jax.sharding import PartitionSpec as P

HD = 128
ROPE_BASE_LOG2 = 8.0
NEG_LARGE = -1e30
F32 = jnp.float32
BF16 = jnp.bfloat16
LOADS = 11
HELP, WORK = 0, 1


def largest_divisor(n):
    best = 1
    for d in range(1, n + 1):
        if n % d == 0 and d * d <= n:
            best = d
    return best


def over(start, count, f):
    if count - start <= 8:
        for o in range(start, count):
            f(o)
    else:
        lax.fori_loop(start, count, lambda o, c: (f(o), c)[1], 0)


class Ring:
    def __init__(self, index, count):
        self.index, self.count = index, count
        self.paired = count & (count - 1) == 0
        self.flips = []
        if self.paired:
            bit = 1
            while bit < count:
                self.flips.append((bit, (1 - 2 * ((index // bit) % 2)) * bit))
                bit *= 2

    def meet(self, o, sign):
        if not self.paired:
            return (self.index + sign * o + self.count) % self.count
        total = self.index
        for bit, flip in self.flips:
            if isinstance(o, int):
                total = total + flip if o & bit else total
            else:
                total = total + flip * ((o // bit) % 2)
        return total

    def to(self, o):
        return self.meet(o, 1)

    def source(self, o):
        return self.meet(o, -1)


def kernel(
    n, heads, img_hbm, txt_hbm, frame_hbm, row_hbm, column_hbm, len_ref, res_hbm, w_hbm, bias_hbm, gate_hbm,
    out_ref, txt_out,
    img_ref, txt_q, places, q_send, k_send, q_all, k_all, v_all, a_send, home, t_send, stage, w, res, bias, gate, total,
    p_send, p_recv, load_sem, k_ss, v_ss, q_ss, x_ss, kr_ss, vr_ss, a_ss, p_ss, t_ss, k_rs, v_rs, q_rs, x_rs, kr_rs, vr_rs,
    a_rs, t1_rs, t3_rs, p_rs,
):
    p = lax.axis_index("seq")
    t = lax.axis_index("tp")
    groups = n // heads
    head = p // groups
    group = p % groups
    tokens = img_ref.shape[1]
    text = txt_hbm.shape[1]
    share = text // groups
    plane_keys = heads * tokens
    early_keys = plane_keys + text
    scale = 1.0 / math.sqrt(HD)
    chunks = p_send.shape[0]
    width = p_send.shape[2]
    half = tokens // 2
    plane = largest_divisor(n)
    lines = n // plane
    inner = largest_divisor(plane)
    outer = plane // inner
    line = p // plane
    v = p % inner
    u = (p // inner) % outer
    near = plane % groups == 0 and groups % inner == 0 and inner % groups == 0
    by_head, by_group = Ring(head, heads), Ring(group, groups)
    by_line, by_u, by_v = Ring(line, lines), Ring(u, outer), Ring(v, inner)
    joined = 2 if by_head.paired and heads % 2 == 0 else heads
    pairs = heads // joined
    by_pair = Ring(head // joined, pairs)

    def on(core):
        return pl.when(t == core)

    def rows(first, count):
        return pl.ds(pl.multiple_of(first, count), count)

    def cols(h):
        return pl.ds(pl.multiple_of(h * HD, HD), HD)

    def plane_slot(j):
        return rows(j * tokens, tokens)

    def relay_slot(o, j):
        return pl.ds(pl.multiple_of(early_keys + ((o - 1) * heads + j) * tokens, tokens), tokens)

    def remote(src, dst, send, recv, seq, core):
        return pltpu.make_async_remote_copy(src, dst, send, recv, device_id={"seq": seq, "tp": core})

    def all_of(count, send, recv):
        if count <= k_all.shape[1]:
            block = k_all.at[0, pl.ds(0, count)]
        else:
            assert count * HD % w.shape[1] == 0
            block = w.at[pl.ds(0, count * HD // w.shape[1])]
        return remote(block, block, send, recv, p, 1 - t)

    barrier = pltpu.get_barrier_semaphore()

    def greet(seq, core):
        pl.semaphore_signal(barrier, inc=1, device_id={"seq": seq, "tp": core})

    def line_up(h):
        return h * groups + group

    def place(l, uu, vv):
        return l * plane + uu * inner + vv

    corners = [(i, k) for i in range(1, outer) for k in range(1, inner)]
    greet(p, 1 - t)
    if near:
        over(1, heads, lambda o: greet(line_up(by_head.to(heads - o)), WORK))
        over(1, groups, lambda o: greet(head * groups + by_group.to(o), WORK))
        for i, k in corners:
            greet(place(line, by_u.to(i), by_v.to(k)), WORK)

        @on(WORK)
        def _():
            over(1, heads, lambda o: greet(line_up(by_head.to(heads - o)), HELP))

        greetings = {WORK: 2 * (heads - 1 + groups - 1 + len(corners)) + 1, HELP: heads}
    else:
        over(1, n, lambda o: greet((p + o) % n, WORK))
        over(1, n, lambda o: greet((p + o) % n, HELP))
        greetings = {WORK: 2 * n - 1, HELP: 2 * n - 1}

    own_text = rows(group * share, share)
    text_keys = pl.ds(plane_keys, text)
    loads = [
        pltpu.make_async_copy(src, dst, load_sem.at[i])
        for i, (src, dst) in enumerate(
            (
                (frame_hbm, places.at[0]),
                (row_hbm, places.at[1]),
                (column_hbm, places.at[2]),
                (img_hbm, img_ref),
                (txt_hbm.at[0, own_text, cols(head)], txt_q.at[WORK]),
                (txt_hbm.at[1, :, cols(head)], k_all.at[WORK, text_keys]),
                (txt_hbm.at[2, :, cols(head)], v_all.at[WORK, text_keys]),
                (w_hbm, w),
                (res_hbm, res),
                (bias_hbm, bias),
                (gate_hbm, gate),
            )
        )
    ]
    for load in loads:
        load.start()

    diagonal = lax.broadcasted_iota(jnp.int32, (tokens, tokens), 0) == lax.broadcasted_iota(
        jnp.int32, (tokens, tokens), 1
    )
    channel = lax.broadcasted_iota(jnp.int32, (1, HD), 1)
    first = HD // 8
    second = (HD - first) // 2
    angles = jnp.zeros((tokens, HD), F32)
    for load in loads[:4]:
        load.wait()
    for part, (start, size) in enumerate(
        ((0, first), (first, second), (first + second, second))
    ):
        inside = (channel >= start) & (channel < start + size)
        pair = ((channel - start) // 2).astype(F32)
        rate = jnp.where(inside, jnp.exp2(pair * (-2.0 * ROPE_BASE_LOG2 / size)), 0.0)
        column = jnp.sum(
            jnp.where(diagonal, places[part].astype(F32), 0.0), axis=1, keepdims=True
        )
        angles = angles + column * rate
    even = lax.broadcasted_iota(jnp.int32, (tokens, HD), 1) % 2 == 0
    cosine = jnp.cos(angles)
    sine = jnp.where(even, -1.0, 1.0) * jnp.sin(angles)
    for which, dst in ((1, k_send), (0, q_send)):
        for h in range(heads):
            x = img_ref[which, :, h * HD : (h + 1) * HD].astype(F32)
            partner = jnp.where(even, pltpu.roll(x, HD - 1, 1), pltpu.roll(x, 1, 1))
            dst[h] = (x * cosine + partner * sine).astype(BF16)

    relayed = (groups - 1) * plane_keys

    def k_copy(o, h, core):
        return remote(k_send.at[h], k_all.at[core, plane_slot(head)], k_ss, k_rs.at[o], line_up(h), WORK)

    def v_copy(o, h, core):
        return remote(img_ref.at[2, :, cols(h)], v_all.at[core, plane_slot(head)], v_ss, v_rs.at[o], line_up(h), WORK)

    def q_copy(o, h, core):
        return remote(q_send.at[h], q_all.at[core, plane_slot(head)], q_ss, q_rs, line_up(h), WORK)

    def finish(count, sem):
        if count:
            all_of(count, sem, sem).wait_send()

    @on(HELP)
    def _():
        pl.semaphore_wait(barrier, greetings[HELP])
        for copy in (k_copy, v_copy, q_copy):
            for o in range(heads):
                copy(o, by_head.to(o), HELP).start()
        remote(txt_hbm.at[0, own_text, cols(head)], txt_q.at[HELP], x_ss, x_rs, p, WORK).start()
        remote(txt_hbm.at[1, :, cols(head)], k_all.at[HELP, text_keys], x_ss, x_rs, p, WORK).start()
        remote(txt_hbm.at[2, :, cols(head)], v_all.at[HELP, text_keys], x_ss, x_rs, p, WORK).start()

    def block(ref, s):
        return ref.at[rows((s % groups) * share, share), cols(s // groups)]

    @on(WORK)
    def _():
        k_all[WORK, plane_slot(head), :] = k_send[head]
        v_all[WORK, plane_slot(head), :] = img_ref[2, :, cols(head)]
        q_all[WORK, plane_slot(head), :] = q_send[head]
        pl.semaphore_wait(barrier, greetings[WORK])
        for copy in (k_copy, v_copy, q_copy):
            for o in range(1, heads):
                copy(o, by_head.to(o), WORK).start()

        def pass_on(data, got, send, recv):
            for o in range(heads):
                j = by_head.source(o)
                all_of((2 if o else 1) * tokens, send, got.at[o]).wait_recv()

                def one(i, j=j):
                    remote(
                        data.at[:, plane_slot(j)], data.at[:, relay_slot(i, j)], send, recv,
                        head * groups + by_group.to(i), WORK,
                    ).start()

                over(1, groups, one)

        pass_on(k_all, k_rs, kr_ss, kr_rs)
        pass_on(v_all, v_rs, vr_ss, vr_rs)
        for load in loads[4:7]:
            load.wait()
        all_of(share + 2 * text, x_ss, x_rs).wait_recv()
        length = len_ref[0]

        def scores_of(queries, core, start, count):
            return lax.dot_general(
                queries, k_all[core, pl.ds(start, count), :], (((1,), (1,)), ((), ())), preferred_element_type=F32
            )

        def early_scores(queries, core):
            scores = scores_of(queries, core, 0, early_keys)
            live = lax.broadcasted_iota(jnp.int32, scores.shape, 1) < plane_keys + length
            return jnp.where(live, scores, NEG_LARGE)

        def weigh(queries, core, scores):
            peak = jnp.max(scores, axis=1, keepdims=True)
            parts = [scores]
            if relayed:
                parts.append(scores_of(queries, core, early_keys, relayed))
                peak = jnp.maximum(peak, jnp.max(parts[1], axis=1, keepdims=True))
            live = lax.broadcasted_iota(jnp.int32, scores.shape, 1) < plane_keys + length
            weights = [jnp.exp((part - peak) * scale) for part in parts]
            weights[0] = jnp.where(live, weights[0], 0.0)
            whole = sum(jnp.sum(part, axis=1, keepdims=True) for part in weights)
            return [part.astype(BF16) for part in weights], whole

        def blend(core, weights, whole):
            mixed = jnp.dot(weights[0], v_all[core, pl.ds(0, early_keys), :], preferred_element_type=F32)
            if relayed:
                mixed = mixed + jnp.dot(
                    weights[1], v_all[core, pl.ds(early_keys, relayed), :], preferred_element_type=F32
                )
            return mixed / whole

        cores = (HELP, WORK)
        text_scores = [early_scores(txt_q[core], core) for core in cores]
        if relayed:
            all_of(2 * relayed, kr_ss, kr_rs).wait_recv()
        text_weights = [weigh(txt_q[core], core, text_scores[core]) for core in cores]
        if relayed:
            all_of(2 * relayed, vr_ss, vr_rs).wait_recv()
        for core in cores:
            done = blend(core, *text_weights[core])
            text_row = lax.broadcasted_iota(jnp.int32, done.shape, 0) + group * share
            done = jnp.where(text_row < length, done, 0.0).astype(BF16)
            t_send[core] = done
            if core == WORK:
                txt_out[own_text, cols(head)] = done
        held = {HELP: stage, WORK: txt_out}
        for o in range(1, lines):
            for core in cores:
                remote(
                    t_send.at[core], block(held[core], p), t_ss.at[0], t1_rs.at[o, core], place(by_line.to(o), u, v), WORK
                ).start()

        members = [(i, k) for i in range(outer) for k in range(inner) if i or k]

        def cross(l, core, own):
            s = place(l, u, v)
            source = t_send.at[core] if own else block(held[core], s)
            for i, k in members:
                remote(
                    source, block(txt_out, s), t_ss.at[1 + core], t3_rs, place(line, by_u.to(i), by_v.to(k)), core
                ).start()
            if core == HELP:
                remote(source, block(txt_out, s), t_ss.at[1 + core], t3_rs, p, core).start()

        for core in cores:
            cross(line, core, True)
        all_of((2 * heads - 1) * tokens, q_ss, q_rs).wait_recv()
        image_weights = [weigh(q_all[core], core, early_scores(q_all[core], core)) for core in cores]
        for core in cores:
            a_send[core] = blend(core, *image_weights[core]).astype(BF16)
        home[:, cols(head)] = a_send[WORK, plane_slot(head), :]
        for o in range(heads):
            j = by_head.to(o)
            for core in cores:
                if o or core == HELP:
                    remote(
                        a_send.at[core, plane_slot(j)], home.at[:, cols(head)], a_ss, a_rs.at[o // joined], line_up(j), core
                    ).start()
        for o in range(1, lines):
            for core in cores:
                all_of(share, t_ss.at[0], t1_rs.at[o, core]).wait_recv()
                cross(by_line.source(o), core, False)

    def project(o):
        @on(HELP)
        def _():
            all_of(joined * tokens, a_ss, a_rs.at[o]).wait_recv()

        @on(WORK)
        def _():
            count = joined * tokens - (tokens if o == 0 else 0)
            if count:
                all_of(count, a_ss, a_rs.at[o]).wait_recv()

        at = rows(by_pair.to(o) * joined * HD, joined * HD)
        return [
            jnp.dot(home[:, at], w[at, c * width : (c + 1) * width], preferred_element_type=F32)
            for c in range(chunks)
        ]

    def p_copy(c):
        return remote(p_send.at[c], p_recv.at[c], p_ss, p_rs.at[c], p, 1 - t)

    for load in loads[7:]:
        load.wait()
    for o in range(pairs - 1):
        for c, part in enumerate(project(o)):
            at = slice(c * width, (c + 1) * width)
            total[:, at] = part if o == 0 else total[:, at] + part
    last = project(pairs - 1)
    mine = []
    for c in range(chunks):
        at = slice(c * width, (c + 1) * width)
        part = last[c] if pairs == 1 else total[:, at] + last[c]
        top, bottom = part[:half], part[half:]
        p_send[c] = jnp.where(t == 0, bottom, top).astype(BF16)
        p_copy(c).start()
        mine.append(jnp.where(t == 0, top, bottom))
    for c in range(chunks):
        at = slice(c * width, (c + 1) * width)
        p_copy(c).wait_recv()
        projected = mine[c] + p_recv[c].astype(F32)
        out_ref[:, at] = (
            res[:, at].astype(F32) + gate[:, at] * (projected + bias[:, at])
        ).astype(BF16)

    @on(HELP)
    def _():
        for load in loads[4:7]:
            load.wait()
        remote(txt_out, txt_out, t_ss.at[0], t3_rs, p, 1 - t).wait_recv()
        for sem in (k_ss, v_ss, q_ss):
            finish(heads * tokens, sem)
        finish(share + 2 * text, x_ss)

    @on(WORK)
    def _():
        if plane > 1:
            all_of(lines * (plane - 1) * share, t_ss.at[0], t3_rs).wait_recv()
        for sem in (k_ss, v_ss, q_ss):
            finish((heads - 1) * tokens, sem)
        finish((2 * heads - 1) * tokens, a_ss)
        finish(2 * relayed, kr_ss)
        finish(2 * relayed, vr_ss)
        finish(2 * (lines - 1) * share, t_ss.at[0])
        remote(txt_out, txt_out, t_ss.at[1 + HELP], t3_rs, p, 1 - t).wait_send()
        finish(lines * (plane - 1) * share, t_ss.at[1 + WORK])

    remote(p_send, p_recv, p_ss, p_rs.at[0], p, 1 - t).wait_send()


def store(img, txt, img_out, txt_out, store_sem):
    stores = [
        pltpu.make_async_copy(a, b.at[0], store_sem.at[i]) for i, (a, b) in enumerate(((txt, txt_out), (img, img_out)))
    ]
    for put in stores:
        put.start()
    for put in stores:
        put.wait()


def shards(img_qkv, txt_qkv, frame_index, row_index, column_index, txt_len, residual, w_proj, proj_bias, gate):
    tokens = img_qkv.shape[1]
    channels = img_qkv.shape[3]
    heads = channels // HD
    n = lax.axis_size("seq")
    groups = n // heads
    text = txt_qkv.shape[1]
    share = text // groups
    lines = n // largest_divisor(n)
    pairs = max(heads // 2, 1)
    model = w_proj.shape[1]
    half = residual.shape[1]
    chunks = 4
    img = img_qkv[0].transpose(1, 0, 2)
    txt = txt_qkv[0].transpose(1, 0, 2)
    hbm = pl.BlockSpec(memory_space=pltpu.HBM)
    vmem = pl.BlockSpec(memory_space=pltpu.VMEM)
    dma = pltpu.SemaphoreType.DMA
    done = pl.pallas_call(
        functools.partial(kernel, n, heads),
        out_shape=(pltpu.VMEM((half, model), BF16), pltpu.VMEM((text, channels), BF16)),
        in_specs=[hbm] * 5 + [pl.BlockSpec(memory_space=pltpu.SMEM)] + [hbm] * 4,
        out_specs=(vmem, vmem),
        scratch_shapes=[
            pltpu.VMEM((3, tokens, channels), BF16),
            pltpu.VMEM((2, share, HD), BF16),
            pltpu.VMEM((3, 1, tokens), jnp.int32),
            pltpu.VMEM((heads, tokens, HD), BF16),
            pltpu.VMEM((heads, tokens, HD), BF16),
            pltpu.VMEM((2, heads * tokens, HD), BF16),
            pltpu.VMEM((2, n * tokens + text, HD), BF16),
            pltpu.VMEM((2, n * tokens + text, HD), BF16),
            pltpu.VMEM((2, heads * tokens, HD), BF16),
            pltpu.VMEM((tokens, channels), BF16),
            pltpu.VMEM((2, share, HD), BF16),
            pltpu.VMEM((text, channels), BF16),
            pltpu.VMEM(w_proj.shape, BF16),
            pltpu.VMEM((half, model), BF16),
            pltpu.VMEM((1, model), F32),
            pltpu.VMEM((1, model), F32),
            pltpu.VMEM((tokens, model), F32),
            pltpu.VMEM((chunks, half, model // chunks), BF16),
            pltpu.VMEM((chunks, half, model // chunks), BF16),
            dma((LOADS,)),
            dma, dma, dma, dma, dma, dma, dma, dma, dma((3,)),
            dma((heads,)), dma((heads,)), dma, dma, dma, dma,
            dma((pairs,)), dma((lines, 2)), dma, dma((chunks,)),
        ],
        compiler_params=pltpu.CompilerParams(
            collective_id=0, has_side_effects=True, vmem_limit_bytes=60000000
        ),
    )(
        img, txt, frame_index, row_index, column_index, txt_len, residual[0], w_proj,
        proj_bias[None], gate[None],
    )
    out, txt_out = (pltpu.with_memory_space_constraint(x, pltpu.VMEM) for x in done)
    return pl.pallas_call(
        store,
        out_shape=(
            jax.ShapeDtypeStruct((1,) + out.shape, BF16),
            jax.ShapeDtypeStruct((1,) + txt_out.shape, BF16),
        ),
        in_specs=[vmem, vmem],
        out_specs=(hbm, hbm),
        scratch_shapes=[dma((2,))],
        compiler_params=pltpu.CompilerParams(vmem_limit_bytes=8000000),
    )(out, txt_out)


def solution(mesh):
    in_specs = (
        P(None, "seq", None, "tp"),
        P(None, None, None, "tp"),
        P(None, "seq"),
        P(None, "seq"),
        P(None, "seq"),
        P(),
        P(None, ("seq", "tp"), None),
        P("tp", None),
        P(),
        P(),
    )
    out_specs = (P(None, ("seq", "tp"), None), P(None, None, "tp"))
    return jax.shard_map(shards, mesh=mesh, in_specs=in_specs, out_specs=out_specs, check_vma=False)
```

time: 25.8 us -> 24.8 us (0.961)
  Pallas kernels: 24.4 us -> 23.3 us
    pallas_call x1, Pallas kernels: 23.5 us -> 22.5 us  [shards(): pl.pallas_call(functools.partial(kernel, n, heads), out_shape=(pltpu.VMEM...]
where the time goes in v2:
time: 24.8 us; the launch traced here: 24.6 us
  Pallas kernels  23.3 us (94%)
  between operations  1.29 us (5%)
    pallas_call x1, Pallas kernels, shards(): pl.pallas_call(functools.partial(kernel, n, heads), out_shape=(pltpu.VMEM...  22.5 us
    pallas_call x1, Pallas kernels, shards(): pl.pallas_call(store, out_shape=(jax.ShapeDtypeStruct((1,) + out.shape, B...  0.83 us

profile of v2, /device:TPU:0, one launch (start us, length us, event | category | flops | bytes accessed | tf_op | source)
XLA Modules:
  0.0 24.6 jit_solution(7570387215586543643)
XLA Ops:
  1.3 22.5 %shard_map.113 = (bf16[16,3072]{1,0:T(8,128)(2,1)S(1)}, bf16[256,1024]{1,0:T(8,128)(2,1)S(1)}) custom-call(bf16[3,32,1024]{2,1,0:T(8,128)(2,1)} %bitcast.10, bf16[3,256,1024]{2,1,0:T(8,128)(2,1)} %bitcast.9, s32[1,32]{1,0:T(1,128)} %frame_hbm.1, s32[1,32]{1,0:T(1,128)} %row_hbm.1, s32[1,32]{1,0:T(1,128)} %column_hbm.1, s32[1]{0:T(128)S(6)} %copy.12.len_ref, ...), custom_call_target="tpu_custom_call" | custom-call | tf_op jit(solution)/shard_map/pallas_call | solution.py:442
  23.8 0.8 %shard_map.114 = (bf16[1,16,3072]{2,1,0:T(8,128)(2,1)}, bf16[1,256,1024]{2,1,0:T(8,128)(2,1)}) custom-call(bf16[16,3072]{1,0:T(8,128)(2,1)S(1)} %get-tuple-element.4.img, bf16[256,1024]{1,0:T(8,128)(2,1)S(1)} %get-tuple-element.5.txt), custom_call_target="tpu_custom_call" | custom-call | tf_op jit(solution)/shard_map/pallas_call | solution.py:480

commit v3 on v2

--- a/solution.py
+++ b/solution.py
@@ -13,7 +13,7 @@
 NEG_LARGE = -1e30
 F32 = jnp.float32
 BF16 = jnp.bfloat16
-LOADS = 11
+LOADS = 6
 HELP, WORK = 0, 1
 
 
@@ -65,8 +65,8 @@
 def kernel(
     n, heads, img_hbm, txt_hbm, frame_hbm, row_hbm, column_hbm, len_ref, res_hbm, w_hbm, bias_hbm, gate_hbm,
     out_ref, txt_out,
-    img_ref, txt_q, places, q_send, k_send, q_all, k_all, v_all, a_send, home, t_send, stage, w, res, bias, gate, total,
-    p_send, p_recv, load_sem, k_ss, v_ss, q_ss, x_ss, kr_ss, vr_ss, a_ss, p_ss, t_ss, k_rs, v_rs, q_rs, x_rs, kr_rs, vr_rs,
+    img_ref, txt_q, places, q_send, k_send, q_all, k_all, v_all, a_send, home, t_send, stage, w, res, scales, total,
+    p_send, p_recv, load_sem, out_ss, relay_ss, p_ss, t_ss, k_rs, v_rs, q_rs, x_rs, kr_rs, vr_rs,
     a_rs, t1_rs, t3_rs, p_rs,
 ):
     p = lax.axis_index("seq")
@@ -118,6 +118,8 @@
     def all_of(count, send, recv):
         if count <= k_all.shape[1]:
             block = k_all.at[0, pl.ds(0, count)]
+        elif count <= 2 * k_all.shape[1] and count % 2 == 0:
+            block = k_all.at[:, pl.ds(0, count // 2)]
         else:
             assert count * HD % w.shape[1] == 0
             block = w.at[pl.ds(0, count * HD // w.shape[1])]
@@ -156,22 +158,27 @@
     text_keys = pl.ds(plane_keys, text)
     loads = [
         pltpu.make_async_copy(src, dst, load_sem.at[i])
-        for i, (src, dst) in enumerate(
-            (
-                (frame_hbm, places.at[0]),
-                (row_hbm, places.at[1]),
-                (column_hbm, places.at[2]),
-                (img_hbm, img_ref),
-                (txt_hbm.at[0, own_text, cols(head)], txt_q.at[WORK]),
-                (txt_hbm.at[1, :, cols(head)], k_all.at[WORK, text_keys]),
-                (txt_hbm.at[2, :, cols(head)], v_all.at[WORK, text_keys]),
-                (w_hbm, w),
-                (res_hbm, res),
-                (bias_hbm, bias),
-                (gate_hbm, gate),
-            )
+        for i, src, dst in (
+            (0, frame_hbm, places.at[0]),
+            (0, row_hbm, places.at[1]),
+            (0, column_hbm, places.at[2]),
+            (1, img_hbm, img_ref),
+            (2, txt_hbm.at[0, own_text, cols(head)], txt_q.at[WORK]),
+            (2, txt_hbm.at[1, :, cols(head)], k_all.at[WORK, text_keys]),
+            (2, txt_hbm.at[2, :, cols(head)], v_all.at[WORK, text_keys]),
+            (3, w_hbm, w),
+            (4, res_hbm, res),
+            (5, bias_hbm, scales.at[0]),
+            (5, gate_hbm, scales.at[1]),
         )
     ]
+
+    def loaded(ref, i):
+        pltpu.make_async_copy(ref, ref, load_sem.at[i]).wait()
+
+    def loaded_text():
+        loaded(k_all.at[WORK, pl.ds(0, share + 2 * text)], 2)
+
     for load in loads:
         load.start()
 
@@ -182,8 +189,8 @@
     first = HD // 8
     second = (HD - first) // 2
     angles = jnp.zeros((tokens, HD), F32)
-    for load in loads[:4]:
-        load.wait()
+    loaded(places, 0)
+    loaded(img_ref, 1)
     for part, (start, size) in enumerate(
         ((0, first), (first, second), (first + second, second))
     ):
@@ -206,13 +213,13 @@
     relayed = (groups - 1) * plane_keys
 
     def k_copy(o, h, core):
-        return remote(k_send.at[h], k_all.at[core, plane_slot(head)], k_ss, k_rs.at[o], line_up(h), WORK)
+        return remote(k_send.at[h], k_all.at[core, plane_slot(head)], out_ss, k_rs.at[o], line_up(h), WORK)
 
     def v_copy(o, h, core):
-        return remote(img_ref.at[2, :, cols(h)], v_all.at[core, plane_slot(head)], v_ss, v_rs.at[o], line_up(h), WORK)
+        return remote(img_ref.at[2, :, cols(h)], v_all.at[core, plane_slot(head)], out_ss, v_rs.at[o], line_up(h), WORK)
 
     def q_copy(o, h, core):
-        return remote(q_send.at[h], q_all.at[core, plane_slot(head)], q_ss, q_rs, line_up(h), WORK)
+        return remote(q_send.at[h], q_all.at[core, plane_slot(head)], out_ss, q_rs, line_up(h), WORK)
 
     def finish(count, sem):
         if count:
@@ -224,9 +231,9 @@
         for copy in (k_copy, v_copy, q_copy):
             for o in range(heads):
                 copy(o, by_head.to(o), HELP).start()
-        remote(txt_hbm.at[0, own_text, cols(head)], txt_q.at[HELP], x_ss, x_rs, p, WORK).start()
-        remote(txt_hbm.at[1, :, cols(head)], k_all.at[HELP, text_keys], x_ss, x_rs, p, WORK).start()
-        remote(txt_hbm.at[2, :, cols(head)], v_all.at[HELP, text_keys], x_ss, x_rs, p, WORK).start()
+        remote(txt_hbm.at[0, own_text, cols(head)], txt_q.at[HELP], out_ss, x_rs, p, WORK).start()
+        remote(txt_hbm.at[1, :, cols(head)], k_all.at[HELP, text_keys], out_ss, x_rs, p, WORK).start()
+        remote(txt_hbm.at[2, :, cols(head)], v_all.at[HELP, text_keys], out_ss, x_rs, p, WORK).start()
 
     def block(ref, s):
         return ref.at[rows((s % groups) * share, share), cols(s // groups)]
@@ -254,11 +261,10 @@
 
                 over(1, groups, one)
 
-        pass_on(k_all, k_rs, kr_ss, kr_rs)
-        pass_on(v_all, v_rs, vr_ss, vr_rs)
-        for load in loads[4:7]:
-            load.wait()
-        all_of(share + 2 * text, x_ss, x_rs).wait_recv()
+        pass_on(k_all, k_rs, relay_ss, kr_rs)
+        pass_on(v_all, v_rs, relay_ss, vr_rs)
+        loaded_text()
+        all_of(share + 2 * text, out_ss, x_rs).wait_recv()
         length = len_ref[0]
 
         def scores_of(queries, core, start, count):
@@ -294,10 +300,10 @@
         cores = (HELP, WORK)
         text_scores = [early_scores(txt_q[core], core) for core in cores]
         if relayed:
-            all_of(2 * relayed, kr_ss, kr_rs).wait_recv()
+            all_of(2 * relayed, relay_ss, kr_rs).wait_recv()
         text_weights = [weigh(txt_q[core], core, text_scores[core]) for core in cores]
         if relayed:
-            all_of(2 * relayed, vr_ss, vr_rs).wait_recv()
+            all_of(2 * relayed, relay_ss, vr_rs).wait_recv()
         for core in cores:
             done = blend(core, *text_weights[core])
             text_row = lax.broadcasted_iota(jnp.int32, done.shape, 0) + group * share
@@ -309,7 +315,7 @@
         for o in range(1, lines):
             for core in cores:
                 remote(
-                    t_send.at[core], block(held[core], p), t_ss.at[0], t1_rs.at[o, core], place(by_line.to(o), u, v), WORK
+                    t_send.at[core], block(held[core], p), t_ss.at[0], t1_rs.at[o - 1, core], place(by_line.to(o), u, v), WORK
                 ).start()
 
         members = [(i, k) for i in range(outer) for k in range(inner) if i or k]
@@ -326,7 +332,7 @@
 
         for core in cores:
             cross(line, core, True)
-        all_of((2 * heads - 1) * tokens, q_ss, q_rs).wait_recv()
+        all_of((2 * heads - 1) * tokens, out_ss, q_rs).wait_recv()
         image_weights = [weigh(q_all[core], core, early_scores(q_all[core], core)) for core in cores]
         for core in cores:
             a_send[core] = blend(core, *image_weights[core]).astype(BF16)
@@ -336,23 +342,23 @@
             for core in cores:
                 if o or core == HELP:
                     remote(
-                        a_send.at[core, plane_slot(j)], home.at[:, cols(head)], a_ss, a_rs.at[o // joined], line_up(j), core
+                        a_send.at[core, plane_slot(j)], home.at[:, cols(head)], out_ss, a_rs.at[o // joined], line_up(j), core
                     ).start()
         for o in range(1, lines):
             for core in cores:
-                all_of(share, t_ss.at[0], t1_rs.at[o, core]).wait_recv()
+                all_of(share, t_ss.at[0], t1_rs.at[o - 1, core]).wait_recv()
                 cross(by_line.source(o), core, False)
 
     def project(o):
         @on(HELP)
         def _():
-            all_of(joined * tokens, a_ss, a_rs.at[o]).wait_recv()
+            all_of(joined * tokens, out_ss, a_rs.at[o]).wait_recv()
 
         @on(WORK)
         def _():
             count = joined * tokens - (tokens if o == 0 else 0)
             if count:
-                all_of(count, a_ss, a_rs.at[o]).wait_recv()
+                all_of(count, out_ss, a_rs.at[o]).wait_recv()
 
         at = rows(by_pair.to(o) * joined * HD, joined * HD)
         return [
@@ -363,8 +369,9 @@
     def p_copy(c):
         return remote(p_send.at[c], p_recv.at[c], p_ss, p_rs.at[c], p, 1 - t)
 
-    for load in loads[7:]:
-        load.wait()
+    loaded(w, 3)
+    loaded(res, 4)
+    loaded(scales, 5)
     for o in range(pairs - 1):
         for c, part in enumerate(project(o)):
             at = slice(c * width, (c + 1) * width)
@@ -383,27 +390,21 @@
         p_copy(c).wait_recv()
         projected = mine[c] + p_recv[c].astype(F32)
         out_ref[:, at] = (
-            res[:, at].astype(F32) + gate[:, at] * (projected + bias[:, at])
+            res[:, at].astype(F32) + scales[1, :, at] * (projected + scales[0, :, at])
         ).astype(BF16)
 
     @on(HELP)
     def _():
-        for load in loads[4:7]:
-            load.wait()
+        loaded_text()
         remote(txt_out, txt_out, t_ss.at[0], t3_rs, p, 1 - t).wait_recv()
-        for sem in (k_ss, v_ss, q_ss):
-            finish(heads * tokens, sem)
-        finish(share + 2 * text, x_ss)
+        finish(3 * heads * tokens + share + 2 * text, out_ss)
 
     @on(WORK)
     def _():
         if plane > 1:
             all_of(lines * (plane - 1) * share, t_ss.at[0], t3_rs).wait_recv()
-        for sem in (k_ss, v_ss, q_ss):
-            finish((heads - 1) * tokens, sem)
-        finish((2 * heads - 1) * tokens, a_ss)
-        finish(2 * relayed, kr_ss)
-        finish(2 * relayed, vr_ss)
+        finish((3 * (heads - 1) + 2 * heads - 1) * tokens, out_ss)
+        finish(4 * relayed, relay_ss)
         finish(2 * (lines - 1) * share, t_ss.at[0])
         remote(txt_out, txt_out, t_ss.at[1 + HELP], t3_rs, p, 1 - t).wait_send()
         finish(lines * (plane - 1) * share, t_ss.at[1 + WORK])
@@ -433,7 +434,7 @@
     pairs = max(heads // 2, 1)
     model = w_proj.shape[1]
     half = residual.shape[1]
-    chunks = 4
+    chunks = 2
     img = img_qkv[0].transpose(1, 0, 2)
     txt = txt_qkv[0].transpose(1, 0, 2)
     hbm = pl.BlockSpec(memory_space=pltpu.HBM)
@@ -459,15 +460,14 @@
             pltpu.VMEM((text, channels), BF16),
             pltpu.VMEM(w_proj.shape, BF16),
             pltpu.VMEM((half, model), BF16),
-            pltpu.VMEM((1, model), F32),
-            pltpu.VMEM((1, model), F32),
+            pltpu.VMEM((2, 1, model), F32),
             pltpu.VMEM((tokens, model), F32),
             pltpu.VMEM((chunks, half, model // chunks), BF16),
             pltpu.VMEM((chunks, half, model // chunks), BF16),
             dma((LOADS,)),
-            dma, dma, dma, dma, dma, dma, dma, dma, dma((3,)),
+            dma, dma, dma, dma((3,)),
             dma((heads,)), dma((heads,)), dma, dma, dma, dma,
-            dma((pairs,)), dma((lines, 2)), dma, dma((chunks,)),
+            dma((pairs,)), dma((max(lines - 1, 1), 2)), dma, dma((chunks,)),
         ],
         compiler_params=pltpu.CompilerParams(
             collective_id=0, has_side_effects=True, vmem_limit_bytes=60000000

time: 24.8 us -> 24.7 us (level)
  no operation moved by 1% of the time
where the time goes in v3:
time: 24.7 us; the launch traced here: 24.5 us
  Pallas kernels  23.2 us (94%)
  between operations  1.29 us (5%)
    pallas_call x1, Pallas kernels, shards(): pl.pallas_call(functools.partial(kernel, n, heads), out_shape=(pltpu.VMEM...  22.4 us
    pallas_call x1, Pallas kernels, shards(): pl.pallas_call(store, out_shape=(jax.ShapeDtypeStruct((1,) + out.shape, B...  0.83 us

profile of v3, /device:TPU:0, one launch (start us, length us, event | category | flops | bytes accessed | tf_op | source)
XLA Modules:
  0.0 24.5 jit_solution(4127680275973656367)
XLA Ops:
  1.3 22.4 %shard_map.113 = (bf16[16,3072]{1,0:T(8,128)(2,1)S(1)}, bf16[256,1024]{1,0:T(8,128)(2,1)S(1)}) custom-call(bf16[3,32,1024]{2,1,0:T(8,128)(2,1)} %bitcast.10, bf16[3,256,1024]{2,1,0:T(8,128)(2,1)} %bitcast.9, s32[1,32]{1,0:T(1,128)} %frame_hbm.1, s32[1,32]{1,0:T(1,128)} %row_hbm.1, s32[1,32]{1,0:T(1,128)} %column_hbm.1, s32[1]{0:T(128)S(6)} %copy.12.len_ref, ...), custom_call_target="tpu_custom_call" | custom-call | tf_op jit(solution)/shard_map/pallas_call | solution.py:443
  23.7 0.8 %shard_map.114 = (bf16[1,16,3072]{2,1,0:T(8,128)(2,1)}, bf16[1,256,1024]{2,1,0:T(8,128)(2,1)}) custom-call(bf16[16,3072]{1,0:T(8,128)(2,1)S(1)} %get-tuple-element.4.img, bf16[256,1024]{1,0:T(8,128)(2,1)S(1)} %get-tuple-element.5.txt), custom_call_target="tpu_custom_call" | custom-call | tf_op jit(solution)/shard_map/pallas_call | solution.py:480
